TPU v7x, 32 devices: a whole 2x2x4 slice. The times are simulated.
32 devices in a mesh: grp: 4 (over x, core), ctx: 8 (over z, y).
Axes of the slice: x: 2, y: 2, z: 4, core: 2. Of those that a mesh axis runs over, the one named last changes fastest.
Arguments:
- queries: bfloat16 [4096, 4096], P(('grp', 'ctx')), parts along dimension 0, may hold values from -8 to 8
- key_states: bfloat16 [4096, 512], P(('grp', 'ctx')), parts along dimension 0, may hold values from -8 to 8
- value_states: bfloat16 [4096, 512], P(('grp', 'ctx')), parts along dimension 0, may hold values from -6 to 6
- grads_out: bfloat16 [4096, 4096], P(('grp', 'ctx')), parts along dimension 0, may hold values from -6 to 6
- doc_lengths: int32 [32], P('grp'), parts along dimension 0, may hold values from 1 to 256, as said below
- block_plan: int32 [64], P('grp'), parts along dimension 0, may hold values from 0 to 15, as said below
- needed: int32 [32, 2], P('grp'), parts along dimension 0, may hold values from 0 to 15, as said below
Outputs:
- outputs: bfloat16 [4096, 4096], P(('grp', 'ctx')), parts along dimension 0
- query_grads: bfloat16 [4096, 4096], P(('grp', 'ctx')), parts along dimension 0
- key_grads: bfloat16 [4096, 512], P(('grp', 'ctx')), parts along dimension 0
- value_grads: bfloat16 [4096, 512], P(('grp', 'ctx')), parts along dimension 0
There are 4 independent parts, one for each index of `grp`. A program takes and returns all parts, laid end to end along the dimension named above; each array names one. Nothing has to cross between parts.
Inputs may be any that keep to these rules, and one draw needn't show every extreme that they name: `doc_lengths`: the lengths sum to 1024 and one of them is exactly 256. `block_plan`: each block position appears once. `needed`: each row lists 2 different stored block numbers, no two of which have the same value of block number // 2.
All inputs are finite; a program needn't handle non-finite values.
Results may differ from a plain program's by a relative error of at most 0.013.
Values may be sent and summed in bfloat16 or wider, within the bound.
A program may use at most 128 MiB of HBM per device.

v0:
```python
import math

import jax
import jax.numpy as jnp
from jax import lax
from jax.sharding import PartitionSpec as P

HEADS = 32
KV_HEADS = 4
HEAD_DIM = 128
BLK = 64


masked_score = -1e30


def token_labels(block_plan, doc_ends, row_start, piece_rows):
    stored = row_start + jnp.arange(piece_rows, dtype=jnp.int32)
    stored_block = stored // BLK
    same_block = stored_block[:, None] == jnp.arange(block_plan.shape[0], dtype=jnp.int32)[None, :]
    placed = jnp.sum(jnp.where(same_block, block_plan[None, :], 0), axis=1) * BLK + stored % BLK
    documents = jnp.sum((doc_ends[None, :] <= placed[:, None]).astype(jnp.int32), axis=1)
    return (stored_block, placed, documents)


def visible(query_labels, key_labels, wanted):
    query_block, query_place, query_doc = query_labels
    key_block, key_place, key_doc = key_labels
    listed = jnp.any(wanted[:, None] == key_block[None, :], axis=0)
    allowed = listed[None, :] | (query_block[:, None] == key_block[None, :])
    return (
        allowed
        & (query_doc[:, None] == key_doc[None, :])
        & (key_place[None, :] <= query_place[:, None])
    )


def forward_step(carried, pieces, row_start, counted, context):
    grouped, query_labels, wanted, block_plan, doc_ends, score_scale = context
    key_piece, value_piece = pieces
    piece_rows = key_piece.shape[0]
    visible_pairs = (
        visible(query_labels, token_labels(block_plan, doc_ends, row_start, piece_rows), wanted)
        & counted
    )

    def forward_update(state_now):
        running_max, running_sum, weighted = state_now
        keys_grouped = key_piece.reshape(piece_rows, KV_HEADS, HEAD_DIM)
        values_wide = value_piece.reshape(piece_rows, KV_HEADS, HEAD_DIM).astype(jnp.float32)
        scores = (
            jnp.einsum("qhgd,khd->hgqk", grouped, keys_grouped, preferred_element_type=jnp.float32)
            * score_scale
        )
        scores = jnp.where(visible_pairs, scores, masked_score)
        new_max = jnp.maximum(running_max, jnp.max(scores, axis=-1))
        weights = jnp.where(visible_pairs, jnp.exp(scores - new_max[..., None]), 0.0)
        factor = jnp.exp(running_max - new_max)
        new_sum = running_sum * factor + jnp.sum(weights, axis=-1)
        product = jnp.einsum(
            "hgqk,khd->hgqd", weights, values_wide, preferred_element_type=jnp.float32
        )
        return (new_max, new_sum, weighted * factor[..., None] + product)

    return lax.cond(jnp.any(visible_pairs), forward_update, lambda state_now: state_now, carried)


def backward_step(carried, pieces, row_start, counted, context):
    (
        grouped,
        query_labels,
        wanted,
        block_plan,
        doc_ends,
        score_scale,
        log_total,
        gradient_rows,
        row_delta,
    ) = context
    key_piece, value_piece = pieces
    piece_rows = key_piece.shape[0]
    visible_pairs = (
        visible(query_labels, token_labels(block_plan, doc_ends, row_start, piece_rows), wanted)
        & counted
    )

    def backward_update(state_now):
        query_acc, pair_grads = state_now
        keys_grouped = key_piece.reshape(piece_rows, KV_HEADS, HEAD_DIM)
        values_grouped = value_piece.reshape(piece_rows, KV_HEADS, HEAD_DIM)
        scores = (
            jnp.einsum("qhgd,khd->hgqk", grouped, keys_grouped, preferred_element_type=jnp.float32)
            * score_scale
        )
        soft_weights = jnp.where(visible_pairs, jnp.exp(scores - log_total[..., None]), 0.0)
        prob_grads = jnp.einsum(
            "qhgd,khd->hgqk", gradient_rows, values_grouped, preferred_element_type=jnp.float32
        )
        score_grads = (soft_weights * (prob_grads - row_delta[..., None])).astype(jnp.bfloat16)
        query_acc = query_acc + jnp.einsum(
            "hgqk,khd->hgqd", score_grads, keys_grouped, preferred_element_type=jnp.float32
        )
        key_part = (
            jnp.einsum("hgqk,qhgd->khd", score_grads, grouped, preferred_element_type=jnp.float32)
            * score_scale
        )
        value_part = jnp.einsum(
            "hgqk,qhgd->khd",
            soft_weights.astype(jnp.bfloat16),
            gradient_rows,
            preferred_element_type=jnp.float32,
        )
        rows_grad = jnp.concatenate(
            [key_part.reshape(piece_rows, -1), value_part.reshape(piece_rows, -1)], axis=1
        )
        current = lax.dynamic_slice_in_dim(pair_grads, row_start, piece_rows, 0)
        pair_grads = lax.dynamic_update_slice_in_dim(pair_grads, current + rows_grad, row_start, 0)
        return (query_acc, pair_grads)

    return lax.cond(jnp.any(visible_pairs), backward_update, lambda state_now: state_now, carried)


def sweep(step_fn, carried, context, own_pieces, own_start, fetch, wanted, own_rank):
    carried = step_fn(carried, own_pieces, own_start, True, context)

    def advance(position, state_now):
        block = wanted[position]
        return step_fn(state_now, fetch(block), block * BLK, block // 2 != own_rank, context)

    return lax.fori_loop(0, wanted.shape[0], advance, carried)


def finish_forward(state_now, grads_out):
    running_max, running_sum, weighted = state_now
    tok_rows = weighted.shape[2]
    attended = weighted / running_sum[..., None]
    outputs = jnp.transpose(attended, (2, 0, 1, 3)).reshape(tok_rows, -1).astype(jnp.bfloat16)
    log_total = running_max + jnp.log(running_sum)
    gradient_rows = grads_out.reshape(tok_rows, KV_HEADS, HEADS // KV_HEADS, HEAD_DIM)
    products = grads_out.astype(jnp.float32) * outputs.astype(jnp.float32)
    summed_rows = jnp.sum(
        products.reshape(tok_rows, KV_HEADS, HEADS // KV_HEADS, HEAD_DIM), axis=-1
    )
    row_delta = jnp.transpose(summed_rows, (1, 2, 0))
    return (outputs, log_total, gradient_rows, row_delta)


def on_device(queries, key_states, value_states, grads_out, doc_lengths, block_plan, needed):
    tok_rows = queries.shape[0]
    group_heads = HEADS // KV_HEADS
    kv_width = KV_HEADS * HEAD_DIM
    ctx_count = lax.axis_size("ctx")
    row_total = tok_rows * ctx_count
    score_scale = 1.0 / math.sqrt(HEAD_DIM)
    doc_ends = jnp.cumsum(doc_lengths)
    own_rank = lax.axis_index("ctx")
    own_start = own_rank * tok_rows
    query_labels = token_labels(block_plan, doc_ends, own_start, tok_rows)
    wanted = lax.dynamic_index_in_dim(needed, own_rank, 0, keepdims=False)
    owner_ids = jnp.arange(ctx_count, dtype=jnp.int32)
    grouped = queries.reshape(tok_rows, KV_HEADS, group_heads, HEAD_DIM)
    stat_shape = (KV_HEADS, group_heads, tok_rows)
    start_state = (
        jnp.full(stat_shape, masked_score, jnp.float32),
        jnp.zeros(stat_shape, jnp.float32),
        jnp.zeros(stat_shape + (HEAD_DIM,), jnp.float32),
    )
    back_start = (
        jnp.zeros(stat_shape + (HEAD_DIM,), jnp.float32),
        jnp.zeros((row_total, 2 * kv_width), jnp.float32),
    )
    forward_context = (grouped, query_labels, wanted, block_plan, doc_ends, score_scale)
    own_pieces = (key_states, value_states)
    request = (needed // 2 == own_rank) & (owner_ids[:, None] != own_rank)
    local_index = jnp.sum(jnp.where(request, needed % 2, 0), axis=1)
    has_request = jnp.any(request, axis=1)

    def pick(member):
        local_blocks = member.reshape(2, BLK, kv_width)
        chosen = jnp.where(
            (local_index == 0)[:, None, None], local_blocks[0][None], local_blocks[1][None]
        )
        return jnp.where(has_request[:, None, None], chosen, jnp.zeros_like(chosen))

    arrived = (
        lax.all_to_all(pick(key_states), "ctx", split_axis=0, concat_axis=0, tiled=True),
        lax.all_to_all(pick(value_states), "ctx", split_axis=0, concat_axis=0, tiled=True),
    )

    def fetch(block):
        return tuple(
            (lax.dynamic_index_in_dim(member, block // 2, 0, keepdims=False) for member in arrived)
        )

    state_now = sweep(
        forward_step, start_state, forward_context, own_pieces, own_start, fetch, wanted, own_rank
    )
    outputs, log_total, gradient_rows, row_delta = finish_forward(state_now, grads_out)
    backward_context = forward_context + (log_total, gradient_rows, row_delta)
    back_state = sweep(
        backward_step, back_start, backward_context, own_pieces, own_start, fetch, wanted, own_rank
    )
    query_acc, pair_grads = back_state
    query_grads = (
        jnp.transpose(query_acc, (2, 0, 1, 3)).reshape(tok_rows, -1) * score_scale
    ).astype(jnp.bfloat16)
    summed = lax.psum_scatter(
        pair_grads.astype(jnp.bfloat16), "ctx", scatter_dimension=0, tiled=True
    ).astype(jnp.float32)
    return (
        outputs,
        query_grads,
        summed[:, :kv_width].astype(jnp.bfloat16),
        summed[:, kv_width:].astype(jnp.bfloat16),
    )


def solution(mesh):
    placed = (
        P(("grp", "ctx"), None),
        P(("grp", "ctx"), None),
        P(("grp", "ctx"), None),
        P(("grp", "ctx"), None),
        P("grp"),
        P("grp"),
        P("grp", None),
    )
    return jax.shard_map(
        on_device,
        mesh=mesh,
        in_specs=placed,
        out_specs=(
            P(("grp", "ctx"), None),
            P(("grp", "ctx"), None),
            P(("grp", "ctx"), None),
            P(("grp", "ctx"), None),
        ),
        check_vma=False,
    )
```

profile of v0, /device:TPU:0, one launch (start us, length us, event | category | flops | bytes accessed | tf_op | source)
XLA Modules:
  0.0 235.7 jit_solution(6708858014378167431)
XLA Ops:
  10.6 21.7 %all_to_all.10 = bf16[8,64,512]{2,1,0:T(8,128)(2,1)} all-to-all(bf16[8,64,512]{2,1,0:T(8,128)(2,1)S(1)} %get-tuple-element.1425), channel_id=1, replica_groups=mesh['grp'=4,'ctx'=8] {'ctx'}, dimensions={0} | all-to-all | bytes 1048576 | tf_op jit(solution)/shard_map/all_to_all | solution.py:186
  32.3 4.1 %all-to-all-start.1 = ((bf16[8,64,512]{2,1,0:T(8,128)(2,1)}), bf16[8,64,512]{2,1,0:T(8,128)(2,1)}, u32[]{:S(2)}, u32[]{:S(2)}) async-start(bf16[8,64,512]{2,1,0:T(8,128)(2,1)} %get-tuple-element.1424), calls=%async_computation.1 | async-start | bytes 1048576 | tf_op jit(solution)/shard_map/all_to_all | solution.py:187
  44.1 8.0 %conditional.4 = (f32[4,8,128]{2,1,0:T(8,128)}, f32[4,8,128]{2,1,0:T(8,128)S(1)}, f32[4,8,128,128]{3,2,1,0:T(8,128)}) conditional(s32[]{:T(128)} %convert_element_type.104, () %tuple.108, (pred[128,128]{0,1:T(8,128)(4,1)S(1)}, bf16[128,512]{1,0:T(8,128)(2,1)S(1)}, bf16[128,4,8,128]{0,3,2,1:T(8,128)(2,1)S(1)}, bf16[128,512]{1,0:T(8,128)(2,1)S(1)}) %tuple.212), branch_computations={%region_5.6_spmd, %region_6.9_spmd} | conditional | flops 275267584 | bytes 18841652 | solution.py:65
  48.1 4.0 %convolution_add_fusion = f32[4,8,128,128]{3,2,1,0:T(8,128)} fusion(f32[4,128,128,8]{2,1,3,0:T(8,128)} %copy-done.7, f32[4,8,128]{2,1,0:T(8,128)S(1)} %get-tuple-element.1396, f32[4,8,128]{2,1,0:T(8,128)} %get-tuple-element.1641, pred[128,128]{0,1:T(8,128)(4,1)S(1)} %get-tuple-element.1030, bf16[128,4,128,1]{2,1,0,3:T(4,128)(2,1)S(1)} %bitcast.154), kind=kOutput, calls=%fused_computation.5 | convolution fusion | flops 136839168 | bytes 4374528 | tf_op jit(solution)/shard_map/cond/branch_1_fun/hgqk,khd->hgqd/dot_general | solution.py:60
  52.1 31.4 %while.40 = (s32[]{:T(128)}, f32[4,8,128]{2,1,0:T(8,128)}, f32[4,8,128]{2,1,0:T(8,128)S(1)}, f32[4,8,128,128]{3,2,1,0:T(8,128)}, s32[2]{0:T(128)}, /*index=5*/s3...) while((s32[]{:T(128)}, f32[4,8,128]{2,1,0:T(8,128)}, ...), condition=%wide.region_20.21_spmd.clone, body=%wide.region_11.20_spmd.clone.sunk | while | flops 137445840 | bytes 9344501 | solution.py:130
  60.8 7.0 %conditional.10 = ((f32[4,8,128]{2,1,0:T(8,128)}, f32[4,8,128]{2,1,0:T(8,128)S(1)}, f32[4,8,128,128]{3,2,1,0:T(8,128)})) conditional(s32[]{:T(128)} %convert_element_type.140, (f32[4,8,128]{2,1,0:T(8,128)}, f32[4,8,128]{2,1,0:T(8,128)S(1)}, f32[4,8,128,128]{3,2,1,0:T(8,128)}) %tuple.179, (pred[128,64]{0,1:T(8,128)(4,1)S(1)}, s32[]{:T(128)}, ...), branch_computations={%region_16.16_spmd, %region_17.19_spmd} | conditional | flops 137371648 | bytes 9330758 | solution.py:65
  63.9 3.2 %multiply_add_fusion = f32[4,8,128,128]{3,2,1,0:T(8,128)} fusion(f32[4,8,128,128]{3,2,1,0:T(8,128)} %get-tuple-element.1040, f32[4,8,128]{2,1,0:T(8,128)S(1)} %get-tuple-element.1399, f32[4,8,128,64]{2,3,1,0:T(8,128)S(1)} %get-tuple-element.1415, f32[4,8,128]{2,1,0:T(8,128)S(1)} %max.5, pred[128,64]{0,1:T(8,128)(4,1)S(1)} %get-tuple-element.1035, ...), kind=kOutput, calls=%fused_computation.21 | convolution fusion | flops 68681728 | bytes 5349376 | tf_op jit(solution)/shard_map/while/body/eval_jaxpr/cond/branch_1_fun/hgqk,khd->hgqd/dot_general | solution.py:60
  76.5 7.0 %conditional.10 = ((f32[4,8,128]{2,1,0:T(8,128)}, f32[4,8,128]{2,1,0:T(8,128)S(1)}, f32[4,8,128,128]{3,2,1,0:T(8,128)})) conditional(s32[]{:T(128)} %convert_element_type.140, (f32[4,8,128]{2,1,0:T(8,128)}, f32[4,8,128]{2,1,0:T(8,128)S(1)}, f32[4,8,128,128]{3,2,1,0:T(8,128)}) %tuple.179, (pred[128,64]{0,1:T(8,128)(4,1)S(1)}, s32[]{:T(128)}, ...), branch_computations={%region_16.16_spmd, %region_17.19_spmd} | conditional | flops 137371648 | bytes 9330758 | solution.py:65
  79.6 3.2 %multiply_add_fusion = f32[4,8,128,128]{3,2,1,0:T(8,128)} fusion(f32[4,8,128,128]{3,2,1,0:T(8,128)} %get-tuple-element.1040, f32[4,8,128]{2,1,0:T(8,128)S(1)} %get-tuple-element.1399, f32[4,8,128,64]{2,3,1,0:T(8,128)S(1)} %get-tuple-element.1415, f32[4,8,128]{2,1,0:T(8,128)S(1)} %max.5, pred[128,64]{0,1:T(8,128)(4,1)S(1)} %get-tuple-element.1035, ...), kind=kOutput, calls=%fused_computation.21 | convolution fusion | flops 68681728 | bytes 5349376 | tf_op jit(solution)/shard_map/while/body/eval_jaxpr/cond/branch_1_fun/hgqk,khd->hgqd/dot_general | solution.py:60
  83.5 2.0 fusion.54
  90.3 2.3 reduce_sum.144
  93.3 24.2 %conditional.5 = (f32[4,8,128,128]{3,2,1,0:T(8,128)}, f32[1024,1024]{1,0:T(8,128)}) conditional(s32[]{:T(128)} %convert_element_type.104, () %tuple.111, (pred[128,128]{0,1:T(8,128)(4,1)}, bf16[128,512]{1,0:T(8,128)(2,1)}, bf16[128,4,8,128]{0,3,2,1:T(8,128)(2,1)S(1)}, f32[4,8,128]{2,1,0:T(8,128)S(1)}, bf16[128,512]{1,0:T(8,128)(2,1)}, ...), branch_computations={%region_22.23_spmd, %region_23.24_spmd} | conditional | flops 674955264 | bytes 52904104 | solution.py:120
  94.2 2.6 %fusion.30 = f32[4,8,128,128]{2,3,1,0:T(8,128)} fusion(bf16[128,4,8,128]{0,3,2,1:T(8,128)(2,1)S(1)} %get-tuple-element.1062, f32[4,8,128]{2,1,0:T(8,128)S(1)} %get-tuple-element.1063, pred[128,128]{0,1:T(8,128)(4,1)} %get-tuple-element.1060, bf16[128,4,128,1]{2,1,0,3:T(4,128)(2,1)S(1)} %bitcast.147), kind=kOutput, calls=%fused_computation.42 | convolution fusion | flops 135790592 | bytes 3309568 | tf_op jit(solution)/shard_map/cond/branch_1_fun/qhgd,khd->hgqk/dot_general | solution.py:92
  99.2 2.5 %fusion.28 = bf16[4,8,128,128]{2,3,1,0:T(8,128)(2,1)S(1)} fusion(f32[4,8,128,128]{2,3,1,0:T(8,128)} %fusion.30, bf16[128,4,8,128]{0,3,2,1:T(8,128)(2,1)} %get-tuple-element.1065, f32[4,8,128]{2,1,0:T(8,128)} %copy.106, bf16[128,4,128,1]{2,1,0,3:T(4,128)(2,1)} %bitcast.153), kind=kOutput, calls=%fused_computation.39 | convolution fusion | flops 135790592 | bytes 4341760 | tf_op jit(solution)/shard_map/cond/branch_1_fun/qhgd,khd->hgqk/dot_general | solution.py:96
  104.1 2.5 %broadcast_in_dim.313 = f32[1024,1024]{0,1:T(8,128)} broadcast(f32[]{:T(128)} %constant.428.clone), dimensions={} | broadcast | bytes 4194308 | tf_op jit(solution)/shard_map/broadcast_in_dim | solution.py:170
  106.6 3.5 %dynamic_update_slice.7 = f32[1024,1024]{0,1:T(8,128)} dynamic-update-slice(f32[1024,1024]{0,1:T(8,128)} %broadcast_in_dim.313, f32[128,1024]{0,1:T(8,128)S(1)} %pad_maximum_fusion, s32[]{:T(128)S(6)} %select_n.302, s32[]{:T(128)} %constant.429.clone) | dynamic-update-slice | bytes 1048580 | tf_op jit(solution)/shard_map/cond/branch_1_fun/dynamic_update_slice | solution.py:117
  110.1 5.4 %copy.154 = f32[1024,1024]{1,0:T(8,128)} copy(f32[1024,1024]{0,1:T(8,128)} %dynamic_update_slice.7) | data formatting | bytes 8388608 | tf_op jit(solution)/shard_map/cond
  117.5 35.9 %while.41 = (s32[]{:T(128)}, f32[4,8,128,128]{3,2,1,0:T(8,128)}, f32[1024,1024]{1,0:T(8,128)}, s32[2]{0:T(128)}, s32[128]{0:T(128)}, /*index=5*/s32[8]{0:T(128)}...) while((s32[]{:T(128)}, f32[4,8,128,128]{3,2,1,0:T(8,128)}, ...), condition=%wide.region_31.32_spmd.clone, body=%wide.region_24.31_spmd.clone.sunk | while | flops 338141664 | bytes 18142832 | solution.py:130
  126.1 9.3 %conditional.11 = ((f32[4,8,128,128]{3,2,1,0:T(8,128)}, f32[1024,1024]{1,0:T(8,128)})) conditional(s32[]{:T(128)} %convert_element_type.142, (f32[4,8,128,128]{3,2,1,0:T(8,128)}, f32[1024,1024]{1,0:T(8,128)}) %tuple.183, (pred[128,64]{0,1:T(8,128)(4,1)S(1)}, s32[]{:T(128)}, bf16[8,64,512]{2,1,0:T(8,128)(2,1)}, ...), branch_computations={%region_29.29_spmd, %region_30.30_spmd} | conditional | flops 338067456 | bytes 18129056 | solution.py:120
  131.8 3.6 %convolution_add_fusion.1 = f32[4,8,128,128]{3,2,1,0:T(8,128)} fusion(f32[4,8,128,128]{3,2,1,0:T(8,128)} %get-tuple-element.1068, bf16[4,8,128,64]{2,3,1,0:T(8,128)(2,1)} %copy-done, bf16[64,4,128,1]{2,1,0,3:T(4,128)(2,1)S(1)} %bitcast.136), kind=kOutput, calls=%fused_computation.52 | convolution fusion | flops 67633152 | bytes 4784128 | tf_op jit(solution)/shard_map/while/body/eval_jaxpr/cond/branch_1_fun/hgqk,khd->hgqd/dot_general | solution.py:100
  144.1 9.3 %conditional.11 = ((f32[4,8,128,128]{3,2,1,0:T(8,128)}, f32[1024,1024]{1,0:T(8,128)})) conditional(s32[]{:T(128)} %convert_element_type.142, (f32[4,8,128,128]{3,2,1,0:T(8,128)}, f32[1024,1024]{1,0:T(8,128)}) %tuple.183, (pred[128,64]{0,1:T(8,128)(4,1)S(1)}, s32[]{:T(128)}, bf16[8,64,512]{2,1,0:T(8,128)(2,1)}, ...), branch_computations={%region_29.29_spmd, %region_30.30_spmd} | conditional | flops 338067456 | bytes 18129056 | solution.py:120
  149.7 3.6 %convolution_add_fusion.1 = f32[4,8,128,128]{3,2,1,0:T(8,128)} fusion(f32[4,8,128,128]{3,2,1,0:T(8,128)} %get-tuple-element.1068, bf16[4,8,128,64]{2,3,1,0:T(8,128)(2,1)} %copy-done, bf16[64,4,128,1]{2,1,0,3:T(4,128)(2,1)S(1)} %bitcast.136), kind=kOutput, calls=%fused_computation.52 | convolution fusion | flops 67633152 | bytes 4784128 | tf_op jit(solution)/shard_map/while/body/eval_jaxpr/cond/branch_1_fun/hgqk,khd->hgqd/dot_general | solution.py:100
  153.4 3.8 %convert_element_type.113 = bf16[1024,1024]{1,0:T(8,128)(2,1)} convert(f32[1024,1024]{1,0:T(8,128)} %get-tuple-element.1121) | non-fusion elementwise | flops 1048576 | bytes 6291456 | tf_op jit(solution)/shard_map/convert_element_type | solution.py:208
  161.3 65.9 %reduce-scatter.2.cloned.1.call-done = bf16[128,1024]{1,0:T(8,128)(2,1)} async-done(((bf16[1024,1024]{1,0:T(8,128)(2,1)}), bf16[128,1024]{1,0:T(8,128)(2,1)}) %reduce-scatter.2.cloned.1.call-update) | async-done | bytes 262160 | tf_op jit(solution)/shard_map/reduce_scatter | solution.py:207
  (159 shorter events, 70.4 us)
Async XLA Ops:
  7.2 29.3 %copy-start.16 = (s32[8,2]{0,1:T(2,128)S(1)}, s32[8,2]{0,1:T(2,128)}, u32[]{:S(2)}) copy-start(s32[8,2]{0,1:T(2,128)} %param.25) | copy-start | bytes 196
  7.2 29.5 %copy-start.18 = (s32[8]{0:T(128)S(1)}, s32[8]{0:T(128)}, u32[]{:S(2)}) copy-start(s32[8]{0:T(128)} %param.23) | copy-start | bytes 100
  32.3 19.8 %all-to-all-start.1 = ((bf16[8,64,512]{2,1,0:T(8,128)(2,1)}), bf16[8,64,512]{2,1,0:T(8,128)(2,1)}, u32[]{:S(2)}, u32[]{:S(2)}) async-start(bf16[8,64,512]{2,1,0:T(8,128)(2,1)} %get-tuple-element.1424), calls=%async_computation.1 | async-start | bytes 1048576 | tf_op jit(solution)/shard_map/all_to_all | solution.py:187
  36.4 190.7 %reduce-scatter.2.cloned.1.call-start = ((), (), s32[]{:S(2)}) async-start(), calls=%async_computation.3 | async-start | bytes 2359296 | tf_op jit(solution)/shard_map/reduce_scatter | solution.py:207
  36.7 2.6 %copy-start.17 = (s32[2]{0:T(128)}, s32[2]{0:T(128)S(1)}, u32[]{:S(2)}) copy-start(s32[2]{0:T(128)S(1)} %dynamic-slice_reduce_fusion) | copy-start | bytes 28
  36.9 2.6 %copy-start.20 = (s32[8,1]{0,1:T(1,128)}, s32[8,1]{0,1:T(1,128)S(1)}, u32[]{:S(2)}) copy-start(s32[8,1]{0,1:T(1,128)S(1)} %reduce-window.8) | copy-start | bytes 100
  36.9 2.5 %copy-start.19 = (s32[16]{0:T(128)S(1)}, s32[16]{0:T(128)}, u32[]{:S(2)}) copy-start(s32[16]{0:T(128)} %param.24) | copy-start | bytes 196
  36.9 4.2 %copy-start.8 = (bf16[128,4096]{1,0:T(8,128)(2,1)S(1)}, bf16[128,4096]{1,0:T(8,128)(2,1)}, u32[]{:S(2)}) copy-start(bf16[128,4096]{1,0:T(8,128)(2,1)} %param.22) | copy-start | bytes 3145732
  38.6 5.5 %copy-start.1 = (bf16[128,4096]{0,1:T(8,128)(2,1)}, bf16[128,4096]{0,1:T(8,128)(2,1)S(1)}, u32[]{:S(2)}) copy-start(bf16[128,4096]{0,1:T(8,128)(2,1)S(1)} %copy.101) | copy-start | bytes 3145732
  38.6 3.8 %copy-start.10 = (bf16[128,512]{1,0:T(8,128)(2,1)S(1)}, bf16[128,512]{1,0:T(8,128)(2,1)}, u32[]{:S(2)}) copy-start(bf16[128,512]{1,0:T(8,128)(2,1)} %param.20) | copy-start | bytes 393220
  38.6 3.8 %copy-start.11 = (bf16[128,512]{1,0:T(8,128)(2,1)S(1)}, bf16[128,512]{1,0:T(8,128)(2,1)}, u32[]{:S(2)}) copy-start(bf16[128,512]{1,0:T(8,128)(2,1)} %param.21) | copy-start | bytes 393220
  39.5 4.6 %copy-start.14 = (s32[128]{0:T(128)}, s32[128]{0:T(128)S(1)}, u32[]{:S(2)}) copy-start(s32[128]{0:T(128)S(1)} %fusion.57) | copy-start | bytes 1540
  39.6 4.5 %copy-start.15 = (s32[128]{0:T(128)}, s32[128]{0:T(128)S(1)}, u32[]{:S(2)}) copy-start(s32[128]{0:T(128)S(1)} %convert_reduce_fusion.2) | copy-start | bytes 1540
  40.4 3.7 %copy-start.13 = (pred[128,128]{0,1:T(8,128)(4,1)}, pred[128,128]{0,1:T(8,128)(4,1)S(1)}, u32[]{:S(2)}) copy-start(pred[128,128]{0,1:T(8,128)(4,1)S(1)} %get-tuple-element.1409) | copy-start | bytes 49156
  44.7 1.4 copy-start.7
  83.5 2.7 %copy-start.9 = (bf16[128,4096]{1,0:T(8,128)(2,1)S(1)}, bf16[128,4096]{1,0:T(8,128)(2,1)}, u32[]{:S(2)}) copy-start(bf16[128,4096]{1,0:T(8,128)(2,1)} %param.22) | copy-start | bytes 3145732
  89.5 3.8 %copy-start.2 = (bf16[128,4096]{0,1:T(8,128)(2,1)S(1)}, bf16[128,4096]{0,1:T(8,128)(2,1)}, u32[]{:S(2)}) copy-start(bf16[128,4096]{0,1:T(8,128)(2,1)} %copy-done.1) | copy-start | bytes 3145732
  99.2 3.4 %copy-start.4 = (bf16[128,4,8,128]{0,3,2,1:T(8,128)(2,1)S(1)}, bf16[128,4,8,128]{0,3,2,1:T(8,128)(2,1)}, u32[]{:S(2)}) copy-start(bf16[128,4,8,128]{0,3,2,1:T(8,128)(2,1)} %get-tuple-element.1065) | copy-start | bytes 3145732 | tf_op jit(solution)/shard_map/cond
  101.7 1.0 copy-start.5
  101.7 2.0 copy-start.3
  110.1 5.4 %copy-start.6 = (bf16[4,8,128,128]{2,3,1,0:T(8,128)(2,1)S(1)}, bf16[4,8,128,128]{2,3,1,0:T(8,128)(2,1)}, u32[]{:S(2)}) copy-start(bf16[4,8,128,128]{2,3,1,0:T(8,128)(2,1)} %copy-done.5) | copy-start | bytes 3145732 | tf_op jit(solution)/shard_map/cond
  126.2 1.5 copy-start.12
  128.1 0.8 copy-start
  144.1 1.5 copy-start.12
  (1 other events, 0.8 us)
Sparse Core Ops, SparseCore 0:
  157.4 69.7 reduce-scatter.1
where the time goes:
time: 237 us; the launch traced here: 236 us
  waiting for transfers between devices  65.9 us (28%)
  local copies, waits for them, and re-layouts  44.2 us (19%)
  other arithmetic  38.3 us (16%)
  matrix products  30.3 us (13%)
  blocking collectives  21.7 us (9%)
  loops' own time  16.1 us (7%)
  between operations  14.9 us (6%)
  starting transfers between devices  4.18 us (2%)
    reduce_scatter x1, waiting for transfers between devices, on_device(): lax.psum_scatter(pair_grads.astype(jnp.bfloat16), 'ctx', scatter_dimensio...  65.9 us
    all_to_all x1, blocking collectives, on_device(): lax.all_to_all(pick(key_states), 'ctx', split_axis=0, concat_axis=0, tile...  21.7 us
    another operation x2, loops' own time, sweep(): return lax.fori_loop(0, wanted.shape[0], advance, carried)  15.7 us
    dot_general x3, matrix products, forward_update(): jnp.einsum('hgqk,khd->hgqd', weights, values_wide, preferred_element_type...  10.5 us
    unnamed x35, local copies, waits for them, and re-layouts  9.26 us
    dot_general x3, matrix products, backward_update(): jnp.einsum('hgqk,khd->hgqd', score_grads, keys_grouped, preferred_element...  9.16 us
    cond x21, local copies, waits for them, and re-layouts  9.11 us
    dynamic_update_slice x3, local copies, waits for them, and re-layouts, backward_update(): lax.dynamic_update_slice_in_dim(pair_grads, current + rows_grad, row_star...  7.18 us
  transfers between devices with their start and end apart: 2, of which 1 were waited for; matrix products, arithmetic and copies ran while one was open for 8% of the time, Pallas kernels for 0%

commit v1 on v0

v1 whole, which is shorter than its diff:
```python
import functools
import math

import jax
import jax.numpy as jnp
from jax import lax
from jax.experimental import pallas as pl
from jax.experimental.pallas import tpu as pltpu
from jax.sharding import PartitionSpec as P

HEADS = 32
KV_HEADS = 4
HEAD_DIM = 128
BLK = 64
GROUP = HEADS // KV_HEADS
CHUNKS = 2
PER_CHUNK = KV_HEADS // CHUNKS
WIDE = 2 * HEAD_DIM * PER_CHUNK
PAIR = 2

masked_score = -1e30


def matmul(a, b, contract):
    return lax.dot_general(
        a, b, ((contract[:1], contract[1:]), ((), ())), preferred_element_type=jnp.float32
    )


def kernel(n, q_hbm, k_ref, v_ref, do_hbm, doc_ref, plan_ref, need_ref, *rest):
    out_hbm, dq_hbm, dk_ref, dv_ref = rest[:4]
    q_buf, do_buf, out_buf, dq_buf, key_acc, value_acc, bias = rest[4:11]
    send, grad_send, grad_recv = rest[11:14]
    recv = rest[14 : 14 + CHUNKS]
    fwd_send, fwd_recv, bwd_send, bwd_recv, load_sem, store_sem = rest[14 + CHUNKS :]
    rows = q_buf.shape[0]
    own_blocks = rows // BLK
    listed_count = need_ref.shape[1]
    me = lax.axis_index("ctx")
    score_scale = 1.0 / math.sqrt(HEAD_DIM)
    chunk_cols = PER_CHUNK * GROUP * HEAD_DIM

    def cols(c):
        return pl.ds(c * chunk_cols, chunk_cols)

    loads, stores, fetches, returns = {}, {}, {}, {}
    for c in range(CHUNKS):
        for i, (src, dst) in enumerate(((q_hbm, q_buf), (do_hbm, do_buf))):
            loads[i, c] = pltpu.make_async_copy(
                src.at[:, cols(c)], dst.at[:, cols(c)], load_sem.at[i, c]
            )
            loads[i, c].start()

    barrier = pltpu.get_barrier_semaphore()
    for o in range(1, n):
        pl.semaphore_signal(
            barrier,
            inc=1,
            device_id={"ctx": lax.rem(me + o, n)},
            device_id_type=pl.DeviceIdType.MESH,
        )

    for o in range(1, n):
        peer = lax.rem(me + o, n)
        half = jnp.int32(0)
        for j in range(listed_count):
            block = need_ref[peer, j]
            half = jnp.where(block // own_blocks == me, block % own_blocks, half)
        keys, values = k_ref[half], v_ref[half]
        for c in range(CHUNKS):
            for i in range(PER_CHUNK):
                g = c * PER_CHUNK + i
                at = slice(g * HEAD_DIM, (g + 1) * HEAD_DIM)
                base = 2 * i * HEAD_DIM
                send[o, c, :, base : base + HEAD_DIM] = keys[:, at]
                send[o, c, :, base + HEAD_DIM : base + 2 * HEAD_DIM] = values[:, at]
    for c in range(CHUNKS):
        recv[c][0] = jnp.zeros((BLK, WIDE), jnp.bfloat16)

    pl.semaphore_wait(barrier, n - 1)
    for c in range(CHUNKS):
        for o in range(1, n):
            fetches[o, c] = pltpu.make_async_remote_copy(
                src_ref=send.at[o, c],
                dst_ref=recv[c].at[o],
                send_sem=fwd_send.at[o, c],
                recv_sem=fwd_recv.at[o, c],
                device_id={"ctx": lax.rem(me + o, n)},
                device_id_type=pl.DeviceIdType.MESH,
            )
            fetches[o, c].start()

    ends, total = [], jnp.int32(0)
    for d in range(doc_ref.shape[0]):
        total = total + doc_ref[d]
        ends.append(total)

    def documents(place):
        doc = jnp.zeros_like(place)
        for end in ends:
            doc = doc + (place >= end).astype(jnp.int32)
        return doc

    key_row = lax.broadcasted_iota(jnp.int32, (BLK, rows), 0)
    query_col = lax.broadcasted_iota(jnp.int32, (BLK, rows), 1)
    query_local = query_col // BLK
    query_place = query_col
    for b in range(own_blocks):
        shift = (plan_ref[me * own_blocks + b] - b) * BLK
        query_place = jnp.where(query_local == b, query_col + shift, query_place)
    query_doc = documents(query_place)
    listed = [need_ref[me, j] for j in range(listed_count)]
    for s in range(own_blocks + listed_count):
        if s < own_blocks:
            block = me * own_blocks + s
            found = jnp.int32(0)
            for b in listed:
                found = jnp.where(b == block, 1, found)
            allowed = jnp.where(query_local == s, 1, found)
        else:
            block = listed[s - own_blocks]
            allowed = jnp.where(block // own_blocks == me, 0, jnp.ones_like(query_col))
        key_place = key_row + plan_ref[block] * BLK
        visible = (allowed > 0) & (documents(key_place) == query_doc) & (key_place <= query_place)
        bias[s * BLK : (s + 1) * BLK, :] = jnp.where(visible, 0.0, masked_score)

    slots = [lax.rem(me - b // own_blocks + n, n) for b in listed]
    exponent = score_scale * math.log2(math.e)

    for c in range(CHUNKS):
        loads[0, c].wait()
        loads[1, c].wait()
        for o in range(1, n):
            fetches[o, c].wait_recv()
        arrived = [recv[c][slot] for slot in slots]
        for i in range(PER_CHUNK):
            g = c * PER_CHUNK + i
            own_at = slice(g * HEAD_DIM, (g + 1) * HEAD_DIM)
            base = 2 * i * HEAD_DIM
            keys = jnp.concatenate(
                [k_ref[b, :, own_at] for b in range(own_blocks)]
                + [piece[:, base : base + HEAD_DIM] for piece in arrived],
                axis=0,
            )
            values = jnp.concatenate(
                [v_ref[b, :, own_at] for b in range(own_blocks)]
                + [piece[:, base + HEAD_DIM : base + 2 * HEAD_DIM] for piece in arrived],
                axis=0,
            )
            keys_t, values_t = keys.T, values.T
            key_grad = value_grad = None
            for p in range(GROUP // PAIR):
                heads = [
                    slice((g * GROUP + p * PAIR + x) * HEAD_DIM, (g * GROUP + p * PAIR + x + 1) * HEAD_DIM)
                    for x in range(PAIR)
                ]
                queries = jnp.concatenate([q_buf[:, at] for at in heads], axis=0)
                grads = jnp.concatenate([do_buf[:, at] for at in heads], axis=0)
                mask = bias[...]
                scores = matmul(keys, queries, (1, 1)) + jnp.concatenate([mask] * PAIR, axis=1)
                highest = jnp.max(scores, axis=0, keepdims=True)
                weights = jnp.exp2((scores - highest) * exponent)
                weights = weights * (1.0 / jnp.sum(weights, axis=0, keepdims=True))
                low = weights.astype(jnp.bfloat16)
                attended = matmul(values_t, low, (1, 0)).T.astype(jnp.bfloat16)
                prob_grads = matmul(values, grads, (1, 1))
                delta = jnp.sum(weights * prob_grads, axis=0, keepdims=True)
                score_grads = (weights * (prob_grads - delta)).astype(jnp.bfloat16)
                query_grad = (matmul(keys_t, score_grads, (1, 0)) * score_scale).T
                query_grad = query_grad.astype(jnp.bfloat16)
                for x, at in enumerate(heads):
                    out_buf[:, at] = attended[x * rows : (x + 1) * rows]
                    dq_buf[:, at] = query_grad[x * rows : (x + 1) * rows]
                more_keys = matmul(score_grads, queries, (1, 0))
                more_values = matmul(low, grads, (1, 0))
                key_grad = more_keys if key_grad is None else key_grad + more_keys
                value_grad = more_values if value_grad is None else value_grad + more_values
            key_grad = key_grad * score_scale
            key_acc[:, own_at] = key_grad[:rows]
            value_acc[:, own_at] = value_grad[:rows]
            for o in range(1, n):
                owner = lax.rem(me - o + n, n)
                for grad, at in ((key_grad, base), (value_grad, base + HEAD_DIM)):
                    piece = jnp.zeros((BLK, HEAD_DIM), jnp.float32)
                    for j, block in enumerate(listed):
                        first = rows + j * BLK
                        piece = jnp.where(
                            block // own_blocks == owner, grad[first : first + BLK], piece
                        )
                    grad_send[o, c, :, at : at + HEAD_DIM] = piece.astype(jnp.bfloat16)
        for o in range(1, n):
            returns[o, c] = pltpu.make_async_remote_copy(
                src_ref=grad_send.at[o, c],
                dst_ref=grad_recv.at[o, c],
                send_sem=bwd_send.at[o, c],
                recv_sem=bwd_recv.at[o, c],
                device_id={"ctx": lax.rem(me - o + n, n)},
                device_id_type=pl.DeviceIdType.MESH,
            )
            returns[o, c].start()
        for i, (src, dst) in enumerate(((out_buf, out_hbm), (dq_buf, dq_hbm))):
            stores[i, c] = pltpu.make_async_copy(
                src.at[:, cols(c)], dst.at[:, cols(c)], store_sem.at[i, c]
            )
            stores[i, c].start()

    for c in range(CHUNKS):
        for o in range(1, n):
            returns[o, c].wait_recv()
        for i in range(PER_CHUNK):
            g = c * PER_CHUNK + i
            own_at = slice(g * HEAD_DIM, (g + 1) * HEAD_DIM)
            base = 2 * i * HEAD_DIM
            for acc, result, at in ((key_acc, dk_ref, base), (value_acc, dv_ref, base + HEAD_DIM)):
                sums = [acc[b * BLK : (b + 1) * BLK, own_at] for b in range(own_blocks)]
                for o in range(1, n):
                    peer = lax.rem(me + o, n)
                    part = grad_recv[o, c, :, at : at + HEAD_DIM].astype(jnp.float32)
                    for b in range(own_blocks):
                        hit = jnp.int32(0)
                        for j in range(listed_count):
                            hit = jnp.where(need_ref[peer, j] == me * own_blocks + b, 1, hit)
                        sums[b] = sums[b] + jnp.where(hit > 0, part, 0.0)
                for b in range(own_blocks):
                    result[b * BLK : (b + 1) * BLK, own_at] = sums[b].astype(jnp.bfloat16)
    for c in range(CHUNKS):
        for o in range(1, n):
            fetches[o, c].wait_send()
            returns[o, c].wait_send()
        stores[0, c].wait()
        stores[1, c].wait()


def on_device(queries, key_states, value_states, grads_out, doc_lengths, block_plan, needed):
    n = lax.axis_size("ctx")
    rows, width = queries.shape
    kv_width = key_states.shape[1]
    blocked = (rows // BLK, BLK, kv_width)
    key_count = rows + needed.shape[1] * BLK
    vmem = pl.BlockSpec(memory_space=pltpu.VMEM)
    smem = pl.BlockSpec(memory_space=pltpu.SMEM)
    anywhere = pl.BlockSpec(memory_space=pl.ANY)
    wide = jax.ShapeDtypeStruct((rows, width), jnp.bfloat16)
    narrow = jax.ShapeDtypeStruct((rows, kv_width), jnp.bfloat16)
    exchange = pltpu.VMEM((n, CHUNKS, BLK, WIDE), jnp.bfloat16)
    dma = pltpu.SemaphoreType.DMA
    return pl.pallas_call(
        functools.partial(kernel, n),
        out_shape=(wide, wide, narrow, narrow),
        in_specs=[anywhere, vmem, vmem, anywhere, smem, smem, smem],
        out_specs=(anywhere, anywhere, vmem, vmem),
        scratch_shapes=[pltpu.VMEM((rows, width), jnp.bfloat16)] * 4
        + [pltpu.VMEM((rows, kv_width), jnp.float32)] * 2
        + [pltpu.VMEM((key_count, rows), jnp.float32)]
        + [exchange] * 3
        + [pltpu.VMEM((n, BLK, WIDE), jnp.bfloat16)] * CHUNKS
        + [dma((n, CHUNKS))] * 4
        + [dma((2, CHUNKS))] * 2,
        compiler_params=pltpu.CompilerParams(collective_id=0, has_side_effects=True),
    )(
        queries,
        key_states.reshape(blocked),
        value_states.reshape(blocked),
        grads_out,
        doc_lengths,
        block_plan,
        needed,
    )


def solution(mesh):
    tokens = P(("grp", "ctx"), None)
    return jax.shard_map(
        on_device,
        mesh=mesh,
        in_specs=(tokens, tokens, tokens, tokens, P("grp"), P("grp"), P("grp", None)),
        out_specs=(tokens, tokens, tokens, tokens),
        check_vma=False,
    )
```

time: 237 us -> 67.6 us (0.29)
  waiting for transfers between devices: 65.9 us -> 0 us
  Pallas kernels: 0 us -> 60.3 us
  other arithmetic: 38.3 us -> 0 us
  local copies, waits for them, and re-layouts: 44.2 us -> 6.35 us
  matrix products: 30.3 us -> 0 us
  blocking collectives: 21.7 us -> 0 us
  loops' own time: 16.1 us -> 0 us
  between operations: 14.9 us -> 0.66 us
  starting transfers between devices: 4.18 us -> 0 us
    reduce_scatter x1 -> x0, waiting for transfers between devices: 65.9 us -> none  [on_device(): lax.psum_scatter(pair_grads.astype(jnp.bfloat16), 'ctx', scatter_dimensio...]
    pallas_call x0 -> x1, Pallas kernels: none -> 60.3 us  [on_device(): pl.pallas_call(functools.partial(kernel, n), out_shape=(wide, wide, narro...]
    dot_general x21 -> x0, matrix products: 30.3 us -> none  [the longest x3 10.5 us: forward_update(): jnp.einsum('hgqk,khd->hgqd', weights, values_wide, preferred_element_type...]
    all_to_all x1 -> x0, blocking collectives: 21.7 us -> none  [on_device(): lax.all_to_all(pick(key_states), 'ctx', split_axis=0, concat_axis=0, tile...]
    another operation x8 -> x0, loops' own time: 16.1 us -> none  [the longest x2 15.7 us: sweep(): return lax.fori_loop(0, wanted.shape[0], advance, carried)]
    reduce_sum x15 -> x0, other arithmetic: 10.6 us -> none  [the longest x5 3.06 us: token_labels(): jnp.sum(jnp.where(same_block, block_plan[None, :], 0), axis=1) * BLK]
    reduce_or x11 -> x0, other arithmetic: 9.97 us -> none  [the longest x3 3.51 us: forward_step(): jnp.any(visible_pairs)]
    cond x21 -> x0, local copies, waits for them, and re-layouts: 9.11 us -> none
  transfers between devices with their start and end apart: 2 -> 0, of which waited for: 1 -> 0; matrix products, arithmetic and copies ran while one was open for 8% -> 0% of each run, Pallas kernels for 0% -> 0%
where the time goes in v1:
time: 67.6 us; the launch traced here: 67.3 us
  Pallas kernels  60.3 us (89%)
  local copies, waits for them, and re-layouts  6.35 us (9%)
    pallas_call x1, Pallas kernels, on_device(): pl.pallas_call(functools.partial(kernel, n), out_shape=(wide, wide, narro...  60.3 us
    unnamed x13, local copies, waits for them, and re-layouts  6.35 us

profile of v1, /device:TPU:0, one launch (start us, length us, event | category | flops | bytes accessed | tf_op | source)
XLA Modules:
  0.0 67.3 jit_solution(3641288104474173037)
XLA Ops:
  0.6 0.0 copy-start.3
  0.6 0.7 copy-done.3
  1.3 0.7 copy.11.need_ref
  2.0 60.3 %shard_map.102 = (bf16[128,4096]{1,0:T(8,128)(2,1)}, bf16[128,4096]{1,0:T(8,128)(2,1)}, bf16[128,512]{1,0:T(8,128)(2,1)}, bf16[128,512]{1,0:T(8,128)(2,1)}) custom-call(bf16[128,4096]{1,0:T(8,128)(2,1)} %q_hbm.1, bf16[2,64,512]{2,1,0:T(8,128)(2,1)} %bitcast.2, bf16[2,64,512]{2,1,0:T(8,128)(2,1)} %bitcast.3, bf16[128,4096]{1,0:T(8,128)(2,1)} %do_hbm.1, ...), custom_call_target="tpu_custom_call" | custom-call | tf_op jit(solution)/shard_map/pallas_call | solution.py:247
  62.3 0.0 copy-start
  62.3 2.4 %copy.16 = bf16[128,4096]{1,0:T(8,128)(2,1)} copy(bf16[128,4096]{1,0:T(8,128)(2,1)} %get-tuple-element.8) | data formatting | bytes 2097152
  64.7 0.0 copy-done
  64.7 0.0 copy-start.2
  64.7 1.0 %copy.17 = bf16[128,4096]{1,0:T(8,128)(2,1)} copy(bf16[128,4096]{1,0:T(8,128)(2,1)S(1)} %copy-done) | data formatting | bytes 2097152
  65.7 0.1 copy-done.2
  65.7 0.0 copy-start.1
  65.7 0.7 copy.18
  66.4 0.3 copy-done.1
  66.7 0.7 copy.19
Async XLA Ops:
  0.6 0.7 %copy-start.3 = (s32[8,2]{0,1:T(2,128)S(1)}, s32[8,2]{0,1:T(2,128)}, u32[]{:S(2)}) copy-start(s32[8,2]{0,1:T(2,128)} %param.13) | copy-start | bytes 196
  62.3 2.4 %copy-start = (bf16[128,4096]{1,0:T(8,128)(2,1)S(1)}, bf16[128,4096]{1,0:T(8,128)(2,1)}, u32[]{:S(2)}) copy-start(bf16[128,4096]{1,0:T(8,128)(2,1)} %get-tuple-element.9) | copy-start | bytes 3145732
  64.7 1.0 %copy-start.2 = (bf16[128,512]{1,0:T(8,128)(2,1)S(1)}, bf16[128,512]{1,0:T(8,128)(2,1)}, u32[]{:S(2)}) copy-start(bf16[128,512]{1,0:T(8,128)(2,1)} %get-tuple-element.10) | copy-start | bytes 393220
  65.7 1.0 %copy-start.1 = (bf16[128,512]{1,0:T(8,128)(2,1)S(1)}, bf16[128,512]{1,0:T(8,128)(2,1)}, u32[]{:S(2)}) copy-start(bf16[128,512]{1,0:T(8,128)(2,1)} %get-tuple-element.11) | copy-start | bytes 393220

commit v2 on v1

--- a/solution.py
+++ b/solution.py
@@ -32,11 +32,17 @@
     q_buf, do_buf, out_buf, dq_buf, key_acc, value_acc, bias = rest[4:11]
     send, grad_send, grad_recv = rest[11:14]
     recv = rest[14 : 14 + CHUNKS]
-    fwd_send, fwd_recv, bwd_send, bwd_recv, load_sem, store_sem = rest[14 + CHUNKS :]
+    relayed = rest[14 + CHUNKS : 14 + 2 * CHUNKS]
+    whole = rest[14 + 2 * CHUNKS]
+    fwd_send, fwd_recv, bwd_send, bwd_recv, load_sem, store_sem = rest[15 + 2 * CHUNKS :]
     rows = q_buf.shape[0]
     own_blocks = rows // BLK
     listed_count = need_ref.shape[1]
     me = lax.axis_index("ctx")
+    side = n // 2
+    local = lax.rem(me, side)
+    side_start = me - local
+    partner = lax.rem(me + side, n)
     score_scale = 1.0 / math.sqrt(HEAD_DIM)
     chunk_cols = PER_CHUNK * GROUP * HEAD_DIM
 
@@ -60,35 +66,52 @@
             device_id_type=pl.DeviceIdType.MESH,
         )
 
-    for o in range(1, n):
-        peer = lax.rem(me + o, n)
+    def near(o):
+        return side_start + lax.rem(local + o, side)
+
+    def half_for(peer, owner):
         half = jnp.int32(0)
         for j in range(listed_count):
             block = need_ref[peer, j]
-            half = jnp.where(block // own_blocks == me, block % own_blocks, half)
+            half = jnp.where(block // own_blocks == owner, block % own_blocks, half)
+        return half
+
+    def pack(keys, values, c):
+        pieces = []
+        for i in range(PER_CHUNK):
+            g = c * PER_CHUNK + i
+            at = slice(g * HEAD_DIM, (g + 1) * HEAD_DIM)
+            pieces += [keys[:, at], values[:, at]]
+        return jnp.concatenate(pieces, axis=1)
+
+    def fetch(key, src, dst, peer, slot, c):
+        fetches[key] = pltpu.make_async_remote_copy(
+            src_ref=src,
+            dst_ref=dst,
+            send_sem=fwd_send.at[slot, c],
+            recv_sem=fwd_recv.at[slot, c],
+            device_id={"ctx": peer},
+            device_id_type=pl.DeviceIdType.MESH,
+        )
+        fetches[key].start()
+
+    for c in range(CHUNKS):
+        for b in range(own_blocks):
+            whole[c, b] = pack(k_ref[b], v_ref[b], c)
+    for o in range(1, side):
+        half = half_for(near(o), me)
         keys, values = k_ref[half], v_ref[half]
         for c in range(CHUNKS):
-            for i in range(PER_CHUNK):
-                g = c * PER_CHUNK + i
-                at = slice(g * HEAD_DIM, (g + 1) * HEAD_DIM)
-                base = 2 * i * HEAD_DIM
-                send[o, c, :, base : base + HEAD_DIM] = keys[:, at]
-                send[o, c, :, base + HEAD_DIM : base + 2 * HEAD_DIM] = values[:, at]
+            send[o, c] = pack(keys, values, c)
     for c in range(CHUNKS):
         recv[c][0] = jnp.zeros((BLK, WIDE), jnp.bfloat16)
 
     pl.semaphore_wait(barrier, n - 1)
     for c in range(CHUNKS):
-        for o in range(1, n):
-            fetches[o, c] = pltpu.make_async_remote_copy(
-                src_ref=send.at[o, c],
-                dst_ref=recv[c].at[o],
-                send_sem=fwd_send.at[o, c],
-                recv_sem=fwd_recv.at[o, c],
-                device_id={"ctx": lax.rem(me + o, n)},
-                device_id_type=pl.DeviceIdType.MESH,
-            )
-            fetches[o, c].start()
+        fetch((0, c), whole.at[c], relayed[c], partner, 0, c)
+    for c in range(CHUNKS):
+        for o in range(1, side):
+            fetch((o, c), send.at[o, c], recv[c].at[o], near(o), o, c)
 
     ends, total = [], jnp.int32(0)
     for d in range(doc_ref.shape[0]):
@@ -124,14 +147,27 @@
         visible = (allowed > 0) & (documents(key_place) == query_doc) & (key_place <= query_place)
         bias[s * BLK : (s + 1) * BLK, :] = jnp.where(visible, 0.0, masked_score)
 
-    slots = [lax.rem(me - b // own_blocks + n, n) for b in listed]
+    for c in range(CHUNKS):
+        fetches[0, c].wait_recv()
+        for o in range(1, side):
+            send[side + o, c] = relayed[c][half_for(near(o), partner)]
+            fetch((side + o, c), send.at[side + o, c], recv[c].at[side + o], near(o), side + o, c)
+        recv[c][side] = relayed[c][half_for(me, partner)]
+
+    slots = []
+    for b in listed:
+        owner = b // own_blocks
+        owner_local = owner % side
+        apart = jnp.where(owner - owner_local == side_start, 0, side)
+        slots.append(lax.rem(local - owner_local + side, side) + apart)
     exponent = score_scale * math.log2(math.e)
 
     for c in range(CHUNKS):
         loads[0, c].wait()
         loads[1, c].wait()
         for o in range(1, n):
-            fetches[o, c].wait_recv()
+            if o != side:
+                fetches[o, c].wait_recv()
         arrived = [recv[c][slot] for slot in slots]
         for i in range(PER_CHUNK):
             g = c * PER_CHUNK + i
@@ -224,9 +260,11 @@
                 for b in range(own_blocks):
                     result[b * BLK : (b + 1) * BLK, own_at] = sums[b].astype(jnp.bfloat16)
     for c in range(CHUNKS):
-        for o in range(1, n):
-            fetches[o, c].wait_send()
-            returns[o, c].wait_send()
+        for o in range(n):
+            if o != side:
+                fetches[o, c].wait_send()
+            if o != 0:
+                returns[o, c].wait_send()
         stores[0, c].wait()
         stores[1, c].wait()
 
@@ -254,6 +292,8 @@
         + [pltpu.VMEM((key_count, rows), jnp.float32)]
         + [exchange] * 3
         + [pltpu.VMEM((n, BLK, WIDE), jnp.bfloat16)] * CHUNKS
+        + [pltpu.VMEM((rows // BLK, BLK, WIDE), jnp.bfloat16)] * CHUNKS
+        + [pltpu.VMEM((CHUNKS, rows // BLK, BLK, WIDE), jnp.bfloat16)]
         + [dma((n, CHUNKS))] * 4
         + [dma((2, CHUNKS))] * 2,
         compiler_params=pltpu.CompilerParams(collective_id=0, has_side_effects=True),

time: 67.6 us -> 59.8 us (0.88)
  Pallas kernels: 60.3 us -> 52.6 us
    pallas_call x1, Pallas kernels: 60.3 us -> 52.6 us  [on_device(): pl.pallas_call(functools.partial(kernel, n), out_shape=(wide, wide, narro...]
where the time goes in v2:
time: 59.8 us; the launch traced here: 59.6 us
  Pallas kernels  52.6 us (88%)
  local copies, waits for them, and re-layouts  6.35 us (11%)
  between operations  0.66 us (1%)
    pallas_call x1, Pallas kernels, on_device(): pl.pallas_call(functools.partial(kernel, n), out_shape=(wide, wide, narro...  52.6 us
    unnamed x13, local copies, waits for them, and re-layouts  6.35 us

profile of v2, /device:TPU:0, one launch (start us, length us, event | category | flops | bytes accessed | tf_op | source)
XLA Modules:
  0.0 59.6 jit_solution(12610533143959502878)
XLA Ops:
  0.6 0.0 copy-start.3
  0.6 0.7 %copy-done.3 = s32[8,2]{0,1:T(2,128)S(1)} copy-done((s32[8,2]{0,1:T(2,128)S(1)}, s32[8,2]{0,1:T(2,128)}, u32[]{:S(2)}) %copy-start.3) | copy-done | bytes 88
  1.3 0.7 %copy.11.need_ref = s32[8,2]{1,0:T(8,128)} copy(s32[8,2]{0,1:T(2,128)S(1)} %copy-done.3) | data formatting | bytes 128 | tf_op args[6]
  2.0 52.6 %shard_map.102 = (bf16[128,4096]{1,0:T(8,128)(2,1)}, bf16[128,4096]{1,0:T(8,128)(2,1)}, bf16[128,512]{1,0:T(8,128)(2,1)}, bf16[128,512]{1,0:T(8,128)(2,1)}) custom-call(bf16[128,4096]{1,0:T(8,128)(2,1)} %q_hbm.1, bf16[2,64,512]{2,1,0:T(8,128)(2,1)} %bitcast.2, bf16[2,64,512]{2,1,0:T(8,128)(2,1)} %bitcast.3, bf16[128,4096]{1,0:T(8,128)(2,1)} %do_hbm.1, ...), custom_call_target="tpu_custom_call" | custom-call | tf_op jit(solution)/shard_map/pallas_call | solution.py:285
  54.6 0.0 copy-start
  54.6 2.4 %copy.16 = bf16[128,4096]{1,0:T(8,128)(2,1)} copy(bf16[128,4096]{1,0:T(8,128)(2,1)} %get-tuple-element.8) | data formatting | bytes 2097152
  57.0 0.0 copy-done
  57.0 0.0 copy-start.2
  57.0 1.0 %copy.17 = bf16[128,4096]{1,0:T(8,128)(2,1)} copy(bf16[128,4096]{1,0:T(8,128)(2,1)S(1)} %copy-done) | data formatting | bytes 2097152
  57.9 0.1 copy-done.2
  58.0 0.0 copy-start.1
  58.0 0.7 %copy.18 = bf16[128,512]{1,0:T(8,128)(2,1)} copy(bf16[128,512]{1,0:T(8,128)(2,1)S(1)} %copy-done.2) | data formatting | bytes 262144
  58.6 0.3 copy-done.1
  58.9 0.7 %copy.19 = bf16[128,512]{1,0:T(8,128)(2,1)} copy(bf16[128,512]{1,0:T(8,128)(2,1)S(1)} %copy-done.1) | data formatting | bytes 262144
Async XLA Ops:
  0.6 0.7 %copy-start.3 = (s32[8,2]{0,1:T(2,128)S(1)}, s32[8,2]{0,1:T(2,128)}, u32[]{:S(2)}) copy-start(s32[8,2]{0,1:T(2,128)} %param.13) | copy-start | bytes 196
  54.6 2.4 %copy-start = (bf16[128,4096]{1,0:T(8,128)(2,1)S(1)}, bf16[128,4096]{1,0:T(8,128)(2,1)}, u32[]{:S(2)}) copy-start(bf16[128,4096]{1,0:T(8,128)(2,1)} %get-tuple-element.9) | copy-start | bytes 3145732
  57.0 1.0 %copy-start.2 = (bf16[128,512]{1,0:T(8,128)(2,1)S(1)}, bf16[128,512]{1,0:T(8,128)(2,1)}, u32[]{:S(2)}) copy-start(bf16[128,512]{1,0:T(8,128)(2,1)} %get-tuple-element.10) | copy-start | bytes 393220
  58.0 1.0 %copy-start.1 = (bf16[128,512]{1,0:T(8,128)(2,1)S(1)}, bf16[128,512]{1,0:T(8,128)(2,1)}, u32[]{:S(2)}) copy-start(bf16[128,512]{1,0:T(8,128)(2,1)} %get-tuple-element.11) | copy-start | bytes 393220

commit v3 on v2

--- a/solution.py
+++ b/solution.py
@@ -33,8 +33,10 @@
     send, grad_send, grad_recv = rest[11:14]
     recv = rest[14 : 14 + CHUNKS]
     relayed = rest[14 + CHUNKS : 14 + 2 * CHUNKS]
-    whole = rest[14 + 2 * CHUNKS]
-    fwd_send, fwd_recv, bwd_send, bwd_recv, load_sem, store_sem = rest[15 + 2 * CHUNKS :]
+    grad_parts = rest[14 + 2 * CHUNKS : 14 + 3 * CHUNKS]
+    grad_relayed = rest[14 + 3 * CHUNKS : 14 + 4 * CHUNKS]
+    whole = rest[14 + 4 * CHUNKS]
+    fwd_send, fwd_recv, bwd_send, bwd_recv, load_sem, store_sem = rest[15 + 4 * CHUNKS :]
     rows = q_buf.shape[0]
     own_blocks = rows // BLK
     listed_count = need_ref.shape[1]
@@ -153,6 +155,23 @@
             send[side + o, c] = relayed[c][half_for(near(o), partner)]
             fetch((side + o, c), send.at[side + o, c], recv[c].at[side + o], near(o), side + o, c)
         recv[c][side] = relayed[c][half_for(me, partner)]
+
+    def part_for(requester, owner):
+        part = jnp.int32(0)
+        for j in range(listed_count):
+            part = jnp.where(need_ref[requester, j] // own_blocks == owner, j, part)
+        return part
+
+    def send_back(key, src, dst, peer, slot, c):
+        returns[key] = pltpu.make_async_remote_copy(
+            src_ref=src,
+            dst_ref=dst,
+            send_sem=bwd_send.at[slot, c],
+            recv_sem=bwd_recv.at[slot, c],
+            device_id={"ctx": peer},
+            device_id_type=pl.DeviceIdType.MESH,
+        )
+        returns[key].start()
 
     slots = []
     for b in listed:
@@ -214,26 +233,17 @@
             key_grad = key_grad * score_scale
             key_acc[:, own_at] = key_grad[:rows]
             value_acc[:, own_at] = value_grad[:rows]
-            for o in range(1, n):
-                owner = lax.rem(me - o + n, n)
-                for grad, at in ((key_grad, base), (value_grad, base + HEAD_DIM)):
-                    piece = jnp.zeros((BLK, HEAD_DIM), jnp.float32)
-                    for j, block in enumerate(listed):
-                        first = rows + j * BLK
-                        piece = jnp.where(
-                            block // own_blocks == owner, grad[first : first + BLK], piece
-                        )
-                    grad_send[o, c, :, at : at + HEAD_DIM] = piece.astype(jnp.bfloat16)
-        for o in range(1, n):
-            returns[o, c] = pltpu.make_async_remote_copy(
-                src_ref=grad_send.at[o, c],
-                dst_ref=grad_recv.at[o, c],
-                send_sem=bwd_send.at[o, c],
-                recv_sem=bwd_recv.at[o, c],
-                device_id={"ctx": lax.rem(me - o + n, n)},
-                device_id_type=pl.DeviceIdType.MESH,
-            )
-            returns[o, c].start()
+            for grad, at in ((key_grad, base), (value_grad, base + HEAD_DIM)):
+                for j in range(listed_count):
+                    first = rows + j * BLK
+                    grad_parts[c][j, :, at : at + HEAD_DIM] = grad[first : first + BLK].astype(
+                        jnp.bfloat16
+                    )
+        send_back((0, c), grad_parts[c], grad_relayed[c], partner, 0, c)
+        for o in range(1, side):
+            owner = near(side - o)
+            grad_send[o, c] = grad_parts[c][part_for(me, owner)]
+            send_back((o, c), grad_send.at[o, c], grad_recv.at[o, c], owner, o, c)
         for i, (src, dst) in enumerate(((out_buf, out_hbm), (dq_buf, dq_hbm))):
             stores[i, c] = pltpu.make_async_copy(
                 src.at[:, cols(c)], dst.at[:, cols(c)], store_sem.at[i, c]
@@ -241,8 +251,17 @@
             stores[i, c].start()
 
     for c in range(CHUNKS):
+        returns[0, c].wait_recv()
+        for o in range(1, side):
+            owner, slot = near(side - o), side + o
+            grad_send[slot, c] = grad_relayed[c][part_for(partner, owner)]
+            send_back((slot, c), grad_send.at[slot, c], grad_recv.at[slot, c], owner, slot, c)
+        grad_recv[side, c] = grad_relayed[c][part_for(partner, me)]
+
+    for c in range(CHUNKS):
         for o in range(1, n):
-            returns[o, c].wait_recv()
+            if o != side:
+                returns[o, c].wait_recv()
         for i in range(PER_CHUNK):
             g = c * PER_CHUNK + i
             own_at = slice(g * HEAD_DIM, (g + 1) * HEAD_DIM)
@@ -250,7 +269,7 @@
             for acc, result, at in ((key_acc, dk_ref, base), (value_acc, dv_ref, base + HEAD_DIM)):
                 sums = [acc[b * BLK : (b + 1) * BLK, own_at] for b in range(own_blocks)]
                 for o in range(1, n):
-                    peer = lax.rem(me + o, n)
+                    peer = near(o) if o < side else lax.rem(near(o - side) + side, n)
                     part = grad_recv[o, c, :, at : at + HEAD_DIM].astype(jnp.float32)
                     for b in range(own_blocks):
                         hit = jnp.int32(0)
@@ -263,7 +282,6 @@
         for o in range(n):
             if o != side:
                 fetches[o, c].wait_send()
-            if o != 0:
                 returns[o, c].wait_send()
         stores[0, c].wait()
         stores[1, c].wait()
@@ -293,6 +311,7 @@
         + [exchange] * 3
         + [pltpu.VMEM((n, BLK, WIDE), jnp.bfloat16)] * CHUNKS
         + [pltpu.VMEM((rows // BLK, BLK, WIDE), jnp.bfloat16)] * CHUNKS
+        + [pltpu.VMEM((needed.shape[1], BLK, WIDE), jnp.bfloat16)] * (2 * CHUNKS)
         + [pltpu.VMEM((CHUNKS, rows // BLK, BLK, WIDE), jnp.bfloat16)]
         + [dma((n, CHUNKS))] * 4
         + [dma((2, CHUNKS))] * 2,

time: 59.8 us -> 55.5 us (0.928)
  Pallas kernels: 52.6 us -> 48.3 us
    pallas_call x1, Pallas kernels: 52.6 us -> 48.3 us  [on_device(): pl.pallas_call(functools.partial(kernel, n), out_shape=(wide, wide, narro...]
where the time goes in v3:
time: 55.5 us; the launch traced here: 55.3 us
  Pallas kernels  48.3 us (87%)
  local copies, waits for them, and re-layouts  6.35 us (11%)
  between operations  0.66 us (1%)
    pallas_call x1, Pallas kernels, on_device(): pl.pallas_call(functools.partial(kernel, n), out_shape=(wide, wide, narro...  48.3 us
    unnamed x13, local copies, waits for them, and re-layouts  6.35 us

profile of v3, /device:TPU:0, one launch (start us, length us, event | category | flops | bytes accessed | tf_op | source)
XLA Modules:
  0.0 55.3 jit_solution(9543617171795174523)
XLA Ops:
  0.6 0.0 copy-start.3
  0.6 0.7 %copy-done.3 = s32[8,2]{0,1:T(2,128)S(1)} copy-done((s32[8,2]{0,1:T(2,128)S(1)}, s32[8,2]{0,1:T(2,128)}, u32[]{:S(2)}) %copy-start.3) | copy-done | bytes 88
  1.3 0.7 %copy.11.need_ref = s32[8,2]{1,0:T(8,128)} copy(s32[8,2]{0,1:T(2,128)S(1)} %copy-done.3) | data formatting | bytes 128 | tf_op args[6]
  2.0 48.3 %shard_map.102 = (bf16[128,4096]{1,0:T(8,128)(2,1)}, bf16[128,4096]{1,0:T(8,128)(2,1)}, bf16[128,512]{1,0:T(8,128)(2,1)}, bf16[128,512]{1,0:T(8,128)(2,1)}) custom-call(bf16[128,4096]{1,0:T(8,128)(2,1)} %q_hbm.1, bf16[2,64,512]{2,1,0:T(8,128)(2,1)} %bitcast.2, bf16[2,64,512]{2,1,0:T(8,128)(2,1)} %bitcast.3, bf16[128,4096]{1,0:T(8,128)(2,1)} %do_hbm.1, ...), custom_call_target="tpu_custom_call" | custom-call | tf_op jit(solution)/shard_map/pallas_call | solution.py:303
  50.3 0.0 copy-start
  50.3 2.4 %copy.16 = bf16[128,4096]{1,0:T(8,128)(2,1)} copy(bf16[128,4096]{1,0:T(8,128)(2,1)} %get-tuple-element.8) | data formatting | bytes 2097152
  52.7 0.0 copy-done
  52.7 0.0 copy-start.2
  52.7 1.0 %copy.17 = bf16[128,4096]{1,0:T(8,128)(2,1)} copy(bf16[128,4096]{1,0:T(8,128)(2,1)S(1)} %copy-done) | data formatting | bytes 2097152
  53.6 0.1 copy-done.2
  53.7 0.0 copy-start.1
  53.7 0.7 %copy.18 = bf16[128,512]{1,0:T(8,128)(2,1)} copy(bf16[128,512]{1,0:T(8,128)(2,1)S(1)} %copy-done.2) | data formatting | bytes 262144
  54.3 0.3 copy-done.1
  54.6 0.7 %copy.19 = bf16[128,512]{1,0:T(8,128)(2,1)} copy(bf16[128,512]{1,0:T(8,128)(2,1)S(1)} %copy-done.1) | data formatting | bytes 262144
Async XLA Ops:
  0.6 0.7 %copy-start.3 = (s32[8,2]{0,1:T(2,128)S(1)}, s32[8,2]{0,1:T(2,128)}, u32[]{:S(2)}) copy-start(s32[8,2]{0,1:T(2,128)} %param.13) | copy-start | bytes 196
  50.3 2.4 %copy-start = (bf16[128,4096]{1,0:T(8,128)(2,1)S(1)}, bf16[128,4096]{1,0:T(8,128)(2,1)}, u32[]{:S(2)}) copy-start(bf16[128,4096]{1,0:T(8,128)(2,1)} %get-tuple-element.9) | copy-start | bytes 3145732
  52.7 1.0 %copy-start.2 = (bf16[128,512]{1,0:T(8,128)(2,1)S(1)}, bf16[128,512]{1,0:T(8,128)(2,1)}, u32[]{:S(2)}) copy-start(bf16[128,512]{1,0:T(8,128)(2,1)} %get-tuple-element.10) | copy-start | bytes 393220
  53.7 1.0 %copy-start.1 = (bf16[128,512]{1,0:T(8,128)(2,1)S(1)}, bf16[128,512]{1,0:T(8,128)(2,1)}, u32[]{:S(2)}) copy-start(bf16[128,512]{1,0:T(8,128)(2,1)} %get-tuple-element.11) | copy-start | bytes 393220
